TPU v7x, 32 devices: a whole 2x2x4 slice. The times are simulated.
32 devices in a mesh: dp: 8 (over z, x), mp: 4 (over y, core).
Axes of the slice: x: 2, y: 2, z: 4, core: 2. Of those that a mesh axis runs over, the one named last changes fastest.
Arguments:
- z_star: bfloat16 [8, 257, 1280], P('dp', None, 'mp'), may hold values from -24 to 24
- cotangent: float32 [8, 257, 1280], P('dp', None, 'mp'), may hold values from -6 to 6
- w_qkv: bfloat16 [3, 1280, 1280], P(None, None, 'mp'), may hold values from -1 to 1
- w_out: bfloat16 [1280, 1280], P('mp'), may hold values from -0.15625 to 0.15625
Outputs:
- implicit: float32 [8, 257, 1280], P('dp', None, 'mp')
- grad_qkv: float32 [3, 1280, 1280], P(None, 'dp', 'mp')
- grad_out: float32 [1280, 1280], P('mp', 'dp')
All inputs are finite; a program needn't handle non-finite values.
Results may differ from a plain program's by a relative error of at most 0.0091.
Values may be sent and summed in bfloat16 or wider, within the bound.
A program may use at most 128 MiB of HBM per device.

v0:
```python
import math

import jax
import jax.numpy as jnp
from jax import lax
from jax.sharding import PartitionSpec as P

HD = 80
TERMS = 3


epsilon = 1e-06


def shards(z_star, cotangent, w_qkv, w_out):
    groups = lax.axis_size("mp")
    images, tokens, narrow = z_star.shape
    model_width = narrow * groups
    columns = w_qkv.shape[2]
    heads_here = columns // HD
    score_scale = HD ** (-0.5)
    position = lax.axis_index("mp")
    whole = lax.all_gather(z_star, "mp", axis=2, tiled=True)
    values = whole.astype(jnp.float32)
    centred = values - jnp.mean(values, axis=-1, keepdims=True)
    inv_std = lax.rsqrt(jnp.mean(centred * centred, axis=-1, keepdims=True) + epsilon)
    normal_f = centred * inv_std
    normal_b = normal_f.astype(jnp.bfloat16)
    flattened = normal_b.reshape(-1, model_width)

    def project(slot_index):
        result = jnp.dot(flattened, w_qkv[slot_index], preferred_element_type=jnp.float32)
        return result.astype(jnp.bfloat16).reshape(images, tokens, heads_here, HD)

    queries = project(0)
    key_vecs = project(1)
    val_vecs = project(2)
    scores = (
        jnp.einsum("bqhe,bkhe->bhqk", queries, key_vecs, preferred_element_type=jnp.float32)
        * score_scale
    )
    attn_probs = jax.nn.softmax(scores, axis=-1)
    probs_b = attn_probs.astype(jnp.bfloat16)
    attended = jnp.einsum("bhqk,bkhe->bqhe", probs_b, val_vecs, preferred_element_type=jnp.float32)
    attended = attended.astype(jnp.bfloat16).reshape(-1, columns)
    contract_first = (((0,), (0,)), ((), ()))
    contract_second = (((1,), (1,)), ((), ()))
    running = cotangent
    gathered = lax.all_gather(cotangent.astype(jnp.bfloat16), "mp", axis=2, tiled=True)
    cot_rows = gathered.reshape(-1, model_width)
    sum_q = None
    sum_o = None
    for term_index in range(TERMS):
        needs_input = term_index + 1 < TERMS
        att_grad = lax.dot_general(
            cot_rows, w_out, contract_second, preferred_element_type=jnp.float32
        )
        att_grad = att_grad.astype(jnp.bfloat16).reshape(images, tokens, heads_here, HD)
        grad_o = lax.dot_general(
            attended, cot_rows, contract_first, preferred_element_type=jnp.float32
        )
        prob_grad = jnp.einsum(
            "bqhe,bkhe->bhqk", att_grad, val_vecs, preferred_element_type=jnp.float32
        )
        rowdot = jnp.sum(attn_probs * prob_grad, axis=-1, keepdims=True)
        score_grad = (attn_probs * (prob_grad - rowdot) * score_scale).astype(jnp.bfloat16)
        q_grad = jnp.einsum(
            "bhqk,bkhe->bqhe", score_grad, key_vecs, preferred_element_type=jnp.float32
        ).astype(jnp.bfloat16)
        k_grad = jnp.einsum(
            "bhqk,bqhe->bkhe", score_grad, queries, preferred_element_type=jnp.float32
        ).astype(jnp.bfloat16)
        v_grad = jnp.einsum(
            "bhqk,bqhe->bkhe", probs_b, att_grad, preferred_element_type=jnp.float32
        ).astype(jnp.bfloat16)
        qkv_grads = [item.reshape(-1, columns) for item in (q_grad, k_grad, v_grad)]
        grad_q = jnp.stack(
            [
                lax.dot_general(flattened, item, contract_first, preferred_element_type=jnp.float32)
                for item in qkv_grads
            ]
        )
        in_part = None
        if needs_input:
            in_part = lax.dot_general(
                qkv_grads[0], w_qkv[0], contract_second, preferred_element_type=jnp.float32
            )
            in_part = in_part + lax.dot_general(
                qkv_grads[1], w_qkv[1], contract_second, preferred_element_type=jnp.float32
            )
            in_part = in_part + lax.dot_general(
                qkv_grads[2], w_qkv[2], contract_second, preferred_element_type=jnp.float32
            )
            in_part = in_part.reshape(images, tokens, model_width)
        grad_q, grad_o, in_part = (grad_q, grad_o, in_part)
        part_q, part_o = (grad_q, grad_o)
        if term_index == 0:
            sum_q, sum_o = (part_q, part_o)
        else:
            sum_q = sum_q + part_q
            sum_o = sum_o + part_o
        if needs_input:
            in_grad = lax.psum(in_part, "mp")
            row_mean = jnp.mean(in_grad, axis=-1, keepdims=True)
            row_dot = jnp.mean(in_grad * normal_f, axis=-1, keepdims=True)
            full_term = (in_grad - row_mean - normal_f * row_dot) * inv_std
            local_term, full_term = (
                lax.dynamic_slice_in_dim(full_term, position * narrow, narrow, 2),
                full_term,
            )
            running = running + local_term
            cot_rows = full_term.astype(jnp.bfloat16).reshape(-1, model_width)
    sum_q, sum_o = (
        lax.psum_scatter(sum_q, "dp", scatter_dimension=1, tiled=True),
        lax.psum_scatter(sum_o, "dp", scatter_dimension=1, tiled=True),
    )
    factor = 1.0 / math.sqrt(images * lax.axis_size("dp") * tokens)
    return (running, sum_q * factor, sum_o * factor)


def solution(mesh):
    return jax.shard_map(
        shards,
        mesh=mesh,
        in_specs=(P("dp", None, "mp"), P("dp", None, "mp"), P(None, None, "mp"), P("mp", None)),
        out_specs=(P("dp", None, "mp"), P(None, "dp", "mp"), P("mp", "dp")),
        check_vma=False,
    )
```

profile of v0, /device:TPU:0, one launch (start us, length us, event | category | flops | bytes accessed | tf_op | source)
XLA Modules:
  0.0 371.2 jit_solution(9127516188160858572)
XLA Ops:
  9.0 17.0 %all_gather.6 = bf16[1,257,1280]{1,0,2:T(2,128)(2,1)} all-gather(bf16[1,257,320]{1,0,2:T(2,128)(2,1)S(1)} %copy.102), channel_id=1, replica_groups=mesh['dp'=8,'mp'=4] {'mp'}, dimensions={2}, use_global_device_ids=true | all-gather | bytes 822400 | tf_op jit(solution)/shard_map/all_gather | solution.py:23
  26.0 3.8 %copy.103 = bf16[1,257,1280]{2,1,0:T(8,128)(2,1)S(1)} copy(bf16[1,257,1280]{1,0,2:T(2,128)(2,1)} %all_gather.6) | data formatting | bytes 1315840 | tf_op jit(solution)/shard_map/all_gather | solution.py:23
  30.3 2.0 convolution_convert_fusion.8
  36.2 15.6 %all_gather.7 = bf16[1,257,1280]{1,0,2:T(2,128)(2,1)} all-gather(bf16[1,257,320]{1,0,2:T(2,128)(2,1)S(1)} %copy.107), channel_id=1, replica_groups=mesh['dp'=8,'mp'=4] {'mp'}, dimensions={2}, use_global_device_ids=true | all-gather | bytes 822400 | tf_op jit(solution)/shard_map/all_gather | solution.py:49
  51.7 3.8 %copy.108 = bf16[1,257,1280]{2,1,0:T(8,128)(2,1)S(1)} copy(bf16[1,257,1280]{1,0,2:T(2,128)(2,1)} %all_gather.7) | data formatting | bytes 1315840 | tf_op jit(solution)/shard_map/all_gather | solution.py:49
  58.0 1.9 exponential_reduce_fusion
  59.9 4.4 %fusion.65 = bf16[4,80,257]{2,1,0:T(8,128)(2,1)} fusion(bf16[257,4,80]{0,2,1:T(8,128)(2,1)S(1)} %bitcast.203, f32[4,257,257]{1,2,0:T(8,128)} %fusion.137, f32[4,257,257]{1,2,0:T(8,128)} %get-tuple-element.23, f32[4,257]{1,0:T(4,128)S(1)} %get-tuple-element.22), kind=kOutput, calls=%fused_computation.64 | convolution fusion | flops 44204256 | bytes 2446640 | tf_op jit(solution)/shard_map/bhqk,bqhe->bkhe/dot_general | solution.py:70
  64.3 4.5 %fusion.62 = bf16[4,80,257]{2,1,0:T(8,128)(2,1)} fusion(bf16[257,4,80]{0,2,1:T(8,128)(2,1)S(1)} %bitcast.208, f32[4,257,257]{1,2,0:T(8,128)} %fusion.137, f32[4,257,257]{1,2,0:T(8,128)} %get-tuple-element.23, f32[4,257]{1,0:T(4,128)S(1)} %get-tuple-element.22), kind=kOutput, calls=%fused_computation.63 | convolution fusion | flops 44204256 | bytes 2446640 | tf_op jit(solution)/shard_map/bhqk,bkhe->bqhe/dot_general | solution.py:67
  75.1 1.9 convolution_bitcast_fusion.6
  77.0 1.9 convolution_bitcast_fusion.7
  79.4 36.4 %all-reduce.3.cloned.1.call-done = f32[1,257,1280]{2,1,0:T(8,128)} async-done(((f32[1,257,1280]{2,1,0:T(8,128)}), f32[1,257,1280]{2,1,0:T(8,128)}) %all-reduce.3.cloned.1.call-update) | async-done | bytes 1315856 | tf_op jit(solution)/shard_map/psum | solution.py:103
  122.1 2.1 convolution_convert_fusion.2
  124.2 2.6 fusion.138
  126.8 4.6 %fusion.56 = bf16[4,80,257]{2,1,0:T(8,128)(2,1)} fusion(bf16[257,4,80]{0,2,1:T(8,128)(2,1)} %bitcast.206, f32[4,257,257]{1,2,0:T(8,128)} %fusion.138, f32[4,257,257]{1,2,0:T(8,128)} %get-tuple-element.23, f32[4,257]{1,0:T(4,128)S(1)} %get-tuple-element.22), kind=kOutput, calls=%fused_computation.61 | convolution fusion | flops 44204256 | bytes 2446640 | tf_op jit(solution)/shard_map/bhqk,bkhe->bqhe/dot_general | solution.py:67
  131.4 4.6 %fusion.59 = bf16[4,80,257]{2,1,0:T(8,128)(2,1)} fusion(bf16[257,4,80]{0,2,1:T(8,128)(2,1)} %bitcast.204, f32[4,257,257]{1,2,0:T(8,128)} %fusion.138, f32[4,257,257]{1,2,0:T(8,128)} %get-tuple-element.23, f32[4,257]{1,0:T(4,128)S(1)} %get-tuple-element.22), kind=kOutput, calls=%fused_computation.62 | convolution fusion | flops 44204256 | bytes 2446640 | tf_op jit(solution)/shard_map/bhqk,bqhe->bkhe/dot_general | solution.py:70
  136.0 1.8 fusion.71
  139.7 2.8 fusion.6
  143.8 2.1 convolution_add_fusion.1
  145.9 36.5 %all-reduce.5.cloned.1.call-done = f32[1,257,1280]{2,1,0:T(8,128)} async-done(((f32[1,257,1280]{2,1,0:T(8,128)}), f32[1,257,1280]{2,1,0:T(8,128)}) %all-reduce.5.cloned.1.call-update) | async-done | bytes 1315856 | tf_op jit(solution)/shard_map/psum | solution.py:103
  186.3 2.1 convolution_add_fusion
  189.3 1.9 convolution_bitcast_fusion.8
  191.2 1.9 convolution_bitcast_fusion.3
  193.1 1.9 convolution_bitcast_fusion.4
  195.1 1.9 convolution_bitcast_fusion.5
  199.4 4.6 %fusion.50 = bf16[4,80,257]{2,1,0:T(8,128)(2,1)} fusion(bf16[257,4,80]{0,2,1:T(8,128)(2,1)S(1)} %bitcast.209, f32[4,257,257]{1,2,0:T(8,128)} %fusion.139, f32[4,257,257]{1,2,0:T(8,128)} %get-tuple-element.23, f32[4,257]{1,0:T(4,128)S(1)} %get-tuple-element.22), kind=kOutput, calls=%fused_computation.59 | convolution fusion | flops 44204256 | bytes 2446640 | tf_op jit(solution)/shard_map/bhqk,bkhe->bqhe/dot_general | solution.py:67
  204.0 2.9 convolution_bitcast_fusion.2
  206.9 3.9 %fusion.53 = bf16[4,80,257]{2,1,0:T(8,128)(2,1)S(1)} fusion(bf16[257,4,80]{0,2,1:T(8,128)(2,1)S(1)} %bitcast.205, f32[4,257,257]{1,2,0:T(8,128)} %fusion.139, f32[4,257,257]{1,2,0:T(8,128)} %get-tuple-element.23, f32[4,257]{1,0:T(4,128)S(1)} %get-tuple-element.22), kind=kOutput, calls=%fused_computation.60 | convolution fusion | flops 44204256 | bytes 2446640 | tf_op jit(solution)/shard_map/bhqk,bqhe->bkhe/dot_general | solution.py:70
  213.6 4.7 %fusion.4 = f32[3,1280,320]{1,2,0:T(8,128)} fusion(f32[1,1280,320]{1,2,0:T(8,128)S(1)} %copy-done.8, f32[1,1280,320]{1,2,0:T(8,128)S(1)} %copy-done.9, f32[1,1280,320]{1,2,0:T(8,128)S(1)} %copy-done.10, f32[1,1280,320]{1,2,0:T(8,128)} %convolution_bitcast_fusion.3, f32[1,1280,320]{1,2,0:T(8,128)} %convolution_bitcast_fusion.4, ...), kind=kLoop, calls=%fused_computation.5 | loop fusion | flops 9830400 | bytes 19660800 | tf_op jit(solution)/shard_map/add | solution.py:100
  218.3 9.1 %copy.136 = f32[3,1280,320]{2,0,1:T(4,128)} copy(f32[3,1280,320]{1,2,0:T(8,128)} %fusion.4) | data formatting | bytes 9830400
  227.4 10.4 %reshape.277 = f32[1280,960]{1,0:T(8,128)} reshape(f32[1280,3,320]{2,1,0:T(4,128)} %bitcast.174) | data formatting | bytes 9830400
  241.4 14.6 %reduce-scatter.5.cloned.1.call-done = f32[320,160]{0,1:T(8,128)} async-done(((f32[320,1280]{0,1:T(8,128)}), f32[320,160]{0,1:T(8,128)}) %reduce-scatter.5.cloned.1.call-update) | async-done | bytes 204816 | tf_op jit(solution)/shard_map/reduce_scatter | solution.py:115
  257.6 103.8 %reduce-scatter.7.cloned.1.call-done = f32[160,960]{1,0:T(8,128)} async-done(((f32[1280,960]{1,0:T(8,128)}), f32[160,960]{1,0:T(8,128)}) %reduce-scatter.7.cloned.1.call-update) | async-done | bytes 614416
  (111 shorter events, 43.0 us)
Async XLA Ops:
  7.2 48.4 %copy-start = (bf16[320,1280]{1,0:T(8,128)(2,1)S(1)}, bf16[320,1280]{1,0:T(8,128)(2,1)}, u32[]{:S(2)}) copy-start(bf16[320,1280]{1,0:T(8,128)(2,1)} %param.7) | copy-start | bytes 2457604
  7.2 108.6 %all-reduce.3.cloned.1.call-start = ((), (), s32[]{:S(2)}) async-start(), calls=%async_computation.2 | async-start | bytes 2703360 | tf_op jit(solution)/shard_map/psum | solution.py:103
  30.0 2.3 copy-start.5
  33.0 1.0 copy-start.16
  35.1 24.8 %copy-start.25 = (bf16[257,320]{0,1:T(8,128)(2,1)}, bf16[257,320]{0,1:T(8,128)(2,1)S(1)}, u32[]{:S(2)}) copy-start(bf16[257,320]{0,1:T(8,128)(2,1)S(1)} %copy.105) | copy-start | bytes 493444
  56.1 1.9 copy-start.27
  56.3 3.6 copy-start.15
  68.8 3.3 copy-start.6
  68.8 3.3 copy-start.18
  70.6 2.0 copy-start.23
  74.9 107.6 %all-reduce.5.cloned.1.call-start = ((), (), s32[]{:S(2)}) async-start(), calls=%async_computation.3 | async-start | bytes 2703360 | tf_op jit(solution)/shard_map/psum | solution.py:103
  75.1 1.9 copy-start.24
  115.8 1.9 copy-start.11
  118.0 1.1 copy-start.1
  136.0 1.9 copy-start.21
  137.9 1.7 copy-start.13
  142.4 113.5 %reduce-scatter.5.cloned.1.call-start = ((), (), s32[]{:S(2)}) async-start(), calls=%async_computation.4 | async-start | bytes 2211840 | tf_op jit(solution)/shard_map/reduce_scatter | solution.py:115
  142.5 1.3 copy-start.2
  182.5 1.9 copy-start.12
  184.3 1.9 copy-start.7
  184.7 1.1 copy-start.3
  188.4 2.8 copy-start.14
  188.4 173.0 %reduce-scatter.7.cloned.1.call-start = ((), (), s32[]{:S(2)}) async-start(), calls=%async_computation.5 | async-start | bytes 5898240
  191.2 1.9 copy-start.22
  193.1 1.9 copy-start.20
  195.1 1.9 copy-start.4
  197.5 1.9 copy-start.28
  204.0 2.9 copy-start.26
  210.8 1.9 copy-start.10
  211.5 1.6 copy-start.8
  211.5 2.0 copy-start.9
  237.8 1.0 copy-start.17
  (1 other events, 0.9 us)
Sparse Core Ops, SparseCore 0:
  75.0 40.6 all-reduce.2
  142.6 39.8 all-reduce.4
  188.5 67.4 reduce-scatter.4
  259.4 101.9 reduce-scatter.6
where the time goes:
time: 372 us; the launch traced here: 371 us
  waiting for transfers between devices  191 us (51%)
  matrix products  74.3 us (20%)
  local copies, waits for them, and re-layouts  43.4 us (12%)
  blocking collectives  32.5 us (9%)
  other arithmetic  14.8 us (4%)
  between operations  14.2 us (4%)
    unnamed x5, waiting for transfers between devices  104 us
    psum x2, waiting for transfers between devices, shards(): in_grad = lax.psum(in_part, 'mp')  72.9 us
    unnamed x66, local copies, waits for them, and re-layouts  31.6 us
    all_gather x1, blocking collectives, shards(): whole = lax.all_gather(z_star, 'mp', axis=2, tiled=True)  17 us
    dot_general x9, matrix products, shards(): lax.dot_general(flattened, item, contract_first, preferred_element_type=j...  15.8 us
    all_gather x1, blocking collectives, shards(): lax.all_gather(cotangent.astype(jnp.bfloat16), 'mp', axis=2, tiled=True)  15.6 us
    reduce_scatter x1, waiting for transfers between devices, shards(): lax.psum_scatter(sum_o, 'dp', scatter_dimension=1, tiled=True)  14.6 us
    dot_general x3, matrix products, shards(): jnp.einsum('bhqk,bkhe->bqhe', score_grad, key_vecs, preferred_element_typ...  13.7 us
  transfers between devices with their start and end apart: 4, of which 4 were waited for; matrix products, arithmetic and copies ran while one was open for 16% of the time, Pallas kernels for 0%

commit v1 on v0

v1 whole, which is shorter than its diff:
```python
import functools
import math

import jax
import jax.numpy as jnp
from jax import lax
from jax.experimental import pallas as pl
from jax.experimental.pallas import tpu as pltpu
from jax.sharding import PartitionSpec as P

HD = 80
TERMS = 3
LANES = 128
MESH = pl.DeviceIdType.MESH


epsilon = 1e-06


def greet(axis, partners):
    barrier = pltpu.get_barrier_semaphore()
    for partner in partners:
        pl.semaphore_signal(barrier, inc=1, device_id={axis: partner}, device_id_type=MESH)
    pl.semaphore_wait(barrier, len(partners))


def remote(src, dst, send, recv, axis, target):
    return pltpu.make_async_remote_copy(
        src_ref=src, dst_ref=dst, send_sem=send, recv_sem=recv,
        device_id={axis: target}, device_id_type=MESH,
    )


def mp_partners():
    me = lax.axis_index("mp")
    core = lax.rem(me, 2)
    return me, core, me + 1 - 2 * core, lax.rem(me + 2, 4)


def gather_kernel(z_ref, cot_ref, nf_ref, nb_ref, inv_ref, cb_ref, cast, z_all, c_all, send, recv):
    me, core, other, across = mp_partners()
    narrow = z_ref.shape[1]
    cast[...] = cot_ref[...].astype(jnp.bfloat16)
    greet("mp", (other, across))
    copies = []
    for k, (src, held) in enumerate(((z_ref, z_all), (cast, c_all))):
        far = remote(src, held.at[me], send.at[k, 0], recv.at[k, 0], "mp", across)
        near = remote(src, held.at[me], send.at[k, 1], recv.at[k, 1], "mp", other)
        far.start()
        near.start()
        copies.append((far, near))

    def finish(k, src, held):
        far, near = copies[k]
        held[me] = src[...]
        far.wait_recv()
        passed = remote(
            held.at[across], held.at[across], send.at[k, 2], recv.at[k, 2], "mp", other
        )
        passed.start()
        near.wait_recv()
        passed.wait_recv()
        far.wait_send()
        near.wait_send()
        passed.wait_send()

    finish(0, z_ref, z_all)
    for s in range(4):
        nf_ref[:, s * narrow : (s + 1) * narrow] = z_all[s].astype(jnp.float32)
    values = nf_ref[...]
    centred = values - jnp.mean(values, axis=-1, keepdims=True)
    inv = lax.rsqrt(jnp.mean(centred * centred, axis=-1, keepdims=True) + epsilon)
    normal = centred * inv
    nf_ref[...] = normal
    nb_ref[...] = normal.astype(jnp.bfloat16)
    inv_ref[...] = inv
    finish(1, cast, c_all)
    for s in range(4):
        cb_ref[:, s * narrow : (s + 1) * narrow] = c_all[s]


def vmem(count):
    return [pl.BlockSpec(memory_space=pltpu.VMEM)] * count


def gather(z, cot):
    tokens, narrow = z.shape
    width = narrow * 4
    held = pltpu.VMEM((4, tokens, narrow), jnp.bfloat16)
    return pl.pallas_call(
        gather_kernel,
        name="gather_mp",
        out_shape=(
            jax.ShapeDtypeStruct((tokens, width), jnp.float32),
            jax.ShapeDtypeStruct((tokens, width), jnp.bfloat16),
            jax.ShapeDtypeStruct((tokens, 1), jnp.float32),
            jax.ShapeDtypeStruct((tokens, width), jnp.bfloat16),
        ),
        in_specs=vmem(2),
        out_specs=tuple(vmem(4)),
        scratch_shapes=[
            pltpu.VMEM((tokens, narrow), jnp.bfloat16),
            held,
            held,
            pltpu.SemaphoreType.DMA((2, 3)),
            pltpu.SemaphoreType.DMA((2, 3)),
        ],
        compiler_params=pltpu.CompilerParams(collective_id=0, has_side_effects=True),
    )(z, cot)


def reduce_kernel(last, part, nf, inv, cb, *refs):
    if last:
        ub_ref, term_ref, a_in, acc, b_out, b_in, c_out, c_in, total, send, recv = refs
    else:
        ub_ref, a_in, acc, b_out, b_in, c_out, c_in, total, send, recv = refs
    me, core, other, across = mp_partners()
    width = part.shape[1]
    half = width // 2
    pieces = half // LANES
    greet("mp", (other, across))

    def columns(which, j):
        return pl.ds(pl.multiple_of(which * half + j * LANES, LANES), LANES)

    first, second, third = [], [], []
    for j in range(pieces):
        copy = remote(
            part.at[:, columns(1 - core, j)], a_in.at[j], send.at[0, j], recv.at[0, j], "mp", other
        )
        copy.start()
        first.append(copy)
    for j in range(pieces):
        first[j].wait_recv()
        summed = part[:, columns(core, j)] + a_in[j]
        acc[j] = summed
        b_out[j] = summed.astype(jnp.bfloat16)
        copy = remote(b_out.at[j], b_in.at[j], send.at[1, j], recv.at[1, j], "mp", across)
        copy.start()
        second.append(copy)
    for j in range(pieces):
        second[j].wait_recv()
        summed = acc[j] + b_in[j].astype(jnp.float32)
        total[core * pieces + j] = summed
        c_out[j] = summed.astype(jnp.bfloat16)
        copy = remote(c_out.at[j], c_in.at[j], send.at[2, j], recv.at[2, j], "mp", other)
        copy.start()
        third.append(copy)
    for j in range(pieces):
        third[j].wait_recv()
        total[(1 - core) * pieces + j] = c_in[j].astype(jnp.float32)
    sums = total[0]
    dots = total[0] * nf[:, :LANES]
    for i in range(1, 2 * pieces):
        sums = sums + total[i]
        dots = dots + total[i] * nf[:, i * LANES : (i + 1) * LANES]
    mean = jnp.sum(sums, axis=-1, keepdims=True) / width
    dot = jnp.sum(dots, axis=-1, keepdims=True) / width
    scale = inv[...]
    for i in range(2 * pieces):
        here = slice(i * LANES, (i + 1) * LANES)
        term = (total[i] - mean - nf[:, here] * dot) * scale
        if last:
            term_ref[:, here] = term
        ub_ref[:, here] = (cb[:, here].astype(jnp.float32) + term).astype(jnp.bfloat16)
    for copy in first + second + third:
        copy.wait_send()


def reduce_norm(part, nf, inv, cb, last, ident):
    tokens, width = part.shape
    pieces = width // 2 // LANES
    shapes = [jax.ShapeDtypeStruct((tokens, width), jnp.bfloat16)]
    if last:
        shapes.append(jax.ShapeDtypeStruct((tokens, width), jnp.float32))
    wide = pltpu.VMEM((pieces, tokens, LANES), jnp.float32)
    slim = pltpu.VMEM((pieces, tokens, LANES), jnp.bfloat16)
    return pl.pallas_call(
        functools.partial(reduce_kernel, last),
        name="reduce_last" if last else "reduce_mid",
        out_shape=tuple(shapes),
        in_specs=vmem(4),
        out_specs=tuple(vmem(len(shapes))),
        scratch_shapes=[
            wide, wide, slim, slim, slim, slim,
            pltpu.VMEM((2 * pieces, tokens, LANES), jnp.float32),
            pltpu.SemaphoreType.DMA((3, pieces)),
            pltpu.SemaphoreType.DMA((3, pieces)),
        ],
        compiler_params=pltpu.CompilerParams(collective_id=ident, has_side_effects=True),
    )(part, nf, inv, cb)


def scatter_kernel(bits, chunks, factor, g_ref, out_ref, *scratch):
    send, recv = scratch[-2:]
    bufs = scratch[:-2]
    me = lax.axis_index("dp")
    mine = [lax.rem(me // (2**b), 2) for b in range(bits)]
    partner = [me + (2**b) * (1 - 2 * mine[b]) for b in range(bits)]
    greet("dp", partner)
    rows = g_ref.shape[-2] // chunks

    def pick(ref, left, b, value, extra):
        where = tuple(value if d == b else slice(None) for d in left)
        return ref.at[where + extra]

    state = []
    for j in range(chunks):
        order = list(range(bits))
        if j % 2 == 1 and bits > 1:
            order[0], order[1] = order[1], order[0]
        state.append(order)
    copies = {}

    def source(j, s):
        left = [d for d in reversed(range(bits)) if d not in state[j][:s]]
        if s == 0:
            return g_ref, left, (pl.ds(j * rows, rows),)
        return bufs[(s - 1) * 2 + 1].at[j], left, ()

    def begin(j, s):
        b = state[j][s]
        ref, left, extra = source(j, s)
        copy = remote(
            pick(ref, left, b, 1 - mine[b], extra), bufs[s * 2].at[j],
            send.at[s, j], recv.at[s, j], "dp", partner[b],
        )
        copy.start()
        copies[s, j] = copy

    def end(j, s):
        b = state[j][s]
        ref, left, extra = source(j, s)
        copies[s, j].wait_recv()
        kept = pick(ref, left, b, mine[b], extra)[...].astype(jnp.float32)
        summed = kept + bufs[s * 2][j].astype(jnp.float32)
        if s == bits - 1:
            out_ref[j * rows : (j + 1) * rows, :] = summed * factor
        else:
            bufs[s * 2 + 1][j] = summed.astype(jnp.bfloat16)
            begin(j, s + 1)

    for j in range(chunks):
        begin(j, 0)
    for step in range(chunks + bits - 1):
        for s in reversed(range(bits)):
            j = step - s
            if 0 <= j < chunks:
                end(j, s)
    for copy in copies.values():
        copy.wait_send()


def scatter(g, ranks, factor):
    bits = ranks.bit_length() - 1
    height, width = g.shape
    block = height // ranks
    chunks = 10 if block % 160 == 0 else 1
    rows = block // chunks
    scratch = []
    for s in range(bits):
        shape = (chunks,) + (2,) * (bits - 1 - s) + (rows, width)
        scratch.append(pltpu.VMEM(shape, jnp.bfloat16))
        scratch.append(pltpu.VMEM(shape, jnp.bfloat16))
    return pl.pallas_call(
        functools.partial(scatter_kernel, bits, chunks, factor),
        name="scatter_dp",
        out_shape=jax.ShapeDtypeStruct((block, width), jnp.float32),
        in_specs=vmem(1),
        out_specs=pl.BlockSpec(memory_space=pltpu.VMEM),
        scratch_shapes=scratch
        + [pltpu.SemaphoreType.DMA((bits, chunks)), pltpu.SemaphoreType.DMA((bits, chunks))],
        compiler_params=pltpu.CompilerParams(collective_id=3, has_side_effects=True),
    )(g.reshape((2,) * bits + (block, width)))


def shards(z_star, cotangent, w_qkv, w_out):
    ranks = lax.axis_size("dp")
    images, tokens, narrow = z_star.shape
    columns = w_qkv.shape[2]
    heads_here = columns // HD
    score_scale = HD ** (-0.5)
    position = lax.axis_index("mp")
    normal_f, flattened, inv_std, cot_rows = gather(z_star[0], cotangent[0])

    def project(slot_index):
        result = jnp.dot(flattened, w_qkv[slot_index], preferred_element_type=jnp.float32)
        return result.astype(jnp.bfloat16).reshape(images, tokens, heads_here, HD)

    queries = project(0)
    key_vecs = project(1)
    val_vecs = project(2)
    scores = (
        jnp.einsum("bqhe,bkhe->bhqk", queries, key_vecs, preferred_element_type=jnp.float32)
        * score_scale
    )
    attn_probs = jax.nn.softmax(scores, axis=-1)
    probs_b = attn_probs.astype(jnp.bfloat16)
    attended = jnp.einsum("bhqk,bkhe->bqhe", probs_b, val_vecs, preferred_element_type=jnp.float32)
    attended = attended.astype(jnp.bfloat16).reshape(-1, columns)
    contract_first = (((0,), (0,)), ((), ()))
    contract_second = (((1,), (1,)), ((), ()))

    def pull_back(rows):
        att_grad = lax.dot_general(rows, w_out, contract_second, preferred_element_type=jnp.float32)
        att_grad = att_grad.astype(jnp.bfloat16).reshape(images, tokens, heads_here, HD)
        prob_grad = jnp.einsum(
            "bqhe,bkhe->bhqk", att_grad, val_vecs, preferred_element_type=jnp.float32
        )
        rowdot = jnp.sum(attn_probs * prob_grad, axis=-1, keepdims=True)
        score_grad = (attn_probs * (prob_grad - rowdot) * score_scale).astype(jnp.bfloat16)
        q_grad = jnp.einsum(
            "bhqk,bkhe->bqhe", score_grad, key_vecs, preferred_element_type=jnp.float32
        ).astype(jnp.bfloat16)
        k_grad = jnp.einsum(
            "bhqk,bqhe->bkhe", score_grad, queries, preferred_element_type=jnp.float32
        ).astype(jnp.bfloat16)
        v_grad = jnp.einsum(
            "bhqk,bqhe->bkhe", probs_b, att_grad, preferred_element_type=jnp.float32
        ).astype(jnp.bfloat16)
        return [item.reshape(-1, columns) for item in (q_grad, k_grad, v_grad)]

    rows = cot_rows
    term = None
    for term_index in range(TERMS - 1):
        grads = pull_back(rows)
        in_part = sum(
            lax.dot_general(grads[c], w_qkv[c], contract_second, preferred_element_type=jnp.float32)
            for c in range(3)
        )
        last = term_index + 2 == TERMS
        made = reduce_norm(in_part, normal_f, inv_std, cot_rows, last, 1 + term_index)
        rows = made[0]
        if last:
            term = made[1]
    implicit = cotangent + lax.dynamic_slice_in_dim(term, position * narrow, narrow, 1)[None]
    grads = pull_back(rows)
    pieces = [
        lax.dot_general(flattened, item, contract_first, preferred_element_type=jnp.float32)
        for item in grads
    ] + [lax.dot_general(rows, attended, contract_first, preferred_element_type=jnp.float32)]
    g = jnp.concatenate([item.astype(jnp.bfloat16) for item in pieces], axis=1)
    factor = 1.0 / math.sqrt(images * ranks * tokens)
    block = scatter(g, ranks, factor)
    grad_qkv = jnp.stack([block[:, c * columns : (c + 1) * columns] for c in range(3)])
    grad_out = block[:, 3 * columns :].T
    return (implicit, grad_qkv, grad_out)


def solution(mesh):
    return jax.shard_map(
        shards,
        mesh=mesh,
        in_specs=(P("dp", None, "mp"), P("dp", None, "mp"), P(None, None, "mp"), P("mp", None)),
        out_specs=(P("dp", None, "mp"), P(None, "dp", "mp"), P("mp", "dp")),
        check_vma=False,
    )
```

time: 372 us -> 204 us (0.55)
  waiting for transfers between devices: 191 us -> 0 us
  Pallas kernels: 0 us -> 115 us
  blocking collectives: 32.5 us -> 0 us
  local copies, waits for them, and re-layouts: 43.4 us -> 18.5 us
  between operations: 14.2 us -> 0.9 us
  matrix products: 74.3 us -> 63.7 us
  other arithmetic: 14.8 us -> 4.24 us
    pallas_call x0 -> x4, Pallas kernels: none -> 115 us  [the longest x1 66.3 us: scatter(): pl.pallas_call(functools.partial(scatter_kernel, bits, chunks, factor), n...]
    unnamed x5 -> x0, waiting for transfers between devices: 104 us -> none
    psum x2 -> x0, waiting for transfers between devices: 72.9 us -> none  [shards(): in_grad = lax.psum(in_part, 'mp')]
    all_gather x2 -> x0, blocking collectives: 32.5 us -> none  [the longest x1 17 us: shards(): whole = lax.all_gather(z_star, 'mp', axis=2, tiled=True)]
    unnamed x66 -> x27, local copies, waits for them, and re-layouts: 31.6 us -> 4.23 us
    reduce_scatter x1 -> x0, waiting for transfers between devices: 14.6 us -> none  [shards(): lax.psum_scatter(sum_o, 'dp', scatter_dimension=1, tiled=True)]
    dot_general x9 -> x3, matrix products: 15.8 us -> 3.73 us  [shards(): lax.dot_general(flattened, item, contract_first, preferred_element_type=j...]
    all_gather x2 -> x0, local copies, waits for them, and re-layouts: 7.57 us -> none  [the longest x1 3.79 us: shards(): whole = lax.all_gather(z_star, 'mp', axis=2, tiled=True)]
  transfers between devices with their start and end apart: 4 -> 0, of which waited for: 4 -> 0; matrix products, arithmetic and copies ran while one was open for 16% -> 0% of each run, Pallas kernels for 0% -> 0%
where the time goes in v1:
time: 204 us; the launch traced here: 203 us
  Pallas kernels  115 us (56%)
  matrix products  63.7 us (31%)
  local copies, waits for them, and re-layouts  18.5 us (9%)
  other arithmetic  4.24 us (2%)
    pallas_call x1, Pallas kernels, scatter(): pl.pallas_call(functools.partial(scatter_kernel, bits, chunks, factor), n...  66.3 us
    pallas_call x2, Pallas kernels, reduce_norm(): pl.pallas_call(functools.partial(reduce_kernel, last), name='reduce_last'...  31.9 us
    pallas_call x1, Pallas kernels, gather(): pl.pallas_call(gather_kernel, name='gather_mp', out_shape=(jax.ShapeDtype...  17.1 us
    dot_general x3, matrix products, pull_back(): jnp.einsum('bhqk,bqhe->bkhe', score_grad, queries, preferred_element_type...  12.9 us
    dot_general x3, matrix products, pull_back(): jnp.einsum('bhqk,bkhe->bqhe', score_grad, key_vecs, preferred_element_typ...  12.9 us
    dot_general x6, matrix products, shards(): lax.dot_general(grads[c], w_qkv[c], contract_second, preferred_element_ty...  11.1 us
    dot_general x3, matrix products, project(): jnp.dot(flattened, w_qkv[slot_index], preferred_element_type=jnp.float32)  6.49 us
    dot_general x3, matrix products, pull_back(): jnp.einsum('bqhe,bkhe->bhqk', att_grad, val_vecs, preferred_element_type=...  5.88 us

profile of v1, /device:TPU:0, one launch (start us, length us, event | category | flops | bytes accessed | tf_op | source)
XLA Modules:
  0.0 202.7 jit_solution(3791085704072291533)
XLA Ops:
  0.6 1.8 copy.65
  2.5 17.1 %gather_mp.1 = (f32[257,1280]{1,0:T(8,128)}, bf16[257,1280]{1,0:T(8,128)(2,1)}, f32[257,1]{1,0:T(8,128)}, bf16[257,1280]{1,0:T(8,128)(2,1)}) custom-call(bf16[257,320]{1,0:T(8,128)(2,1)} %bitcast.165, f32[257,320]{1,0:T(8,128)} %bitcast.146), custom_call_target="tpu_custom_call" | custom-call | tf_op jit(solution)/shard_map/gather_mp/pallas_call | solution.py:90
  19.6 1.9 convolution_convert_fusion.13
  22.4 2.3 %convolution_convert_fusion.12 = bf16[257,320]{1,0:T(8,128)(2,1)} fusion(bf16[257,1280]{1,0:T(8,128)(2,1)} %get-tuple-element.9, bf16[3,1280,320]{1,2,0:T(8,128)(2,1)S(1)} %copy-done.1), kind=kOutput, calls=%fused_computation.47 | convolution fusion | flops 210616640 | bytes 1641600 | tf_op jit(solution)/shard_map/dot_general | solution.py:287
  25.8 2.9 %exponential_reduce_fusion = (f32[4,257]{1,0:T(4,128)S(1)}, f32[4,257,257]{1,2,0:T(8,128)}) fusion(bf16[257,4,80]{0,2,1:T(8,128)(2,1)S(1)} %bitcast.151, bf16[257,4,80]{0,2,1:T(8,128)(2,1)} %bitcast.155), kind=kOutput, calls=%fused_computation.30 | convolution fusion | flops 43064204 | bytes 1389856 | tf_op jit(solution)/shard_map/sub | solution.py:297
  28.7 2.3 %convolution_convert_fusion.10 = bf16[257,320]{1,0:T(8,128)(2,1)} fusion(bf16[257,1280]{1,0:T(8,128)(2,1)} %get-tuple-element.9, bf16[3,1280,320]{1,2,0:T(8,128)(2,1)S(1)} %copy-done.1), kind=kOutput, calls=%fused_computation.45 | convolution fusion | flops 210616640 | bytes 1641600 | tf_op jit(solution)/shard_map/dot_general | solution.py:287
  32.2 2.3 %convolution_convert_fusion.11 = bf16[257,320]{1,0:T(8,128)(2,1)} fusion(bf16[257,1280]{1,0:T(8,128)(2,1)} %get-tuple-element.10.cb, bf16[320,1280]{1,0:T(8,128)(2,1)S(1)} %copy-done), kind=kOutput, calls=%fused_computation.46 | convolution fusion | flops 210616640 | bytes 1641600 | tf_op jit(solution)/shard_map/dot_general | solution.py:305
  34.5 1.8 copy.38
  36.3 2.6 %fusion.94 = f32[4,257,257]{1,2,0:T(8,128)} fusion(bf16[257,4,80]{0,2,1:T(8,128)(2,1)} %bitcast.142, bf16[257,4,80]{0,2,1:T(8,128)(2,1)S(1)} %bitcast.136), kind=kOutput, calls=%fused_computation.99 | convolution fusion | flops 42271360 | bytes 1385744 | tf_op jit(solution)/shard_map/bqhe,bkhe->bhqk/dot_general | solution.py:307
  38.9 4.6 %fusion.48 = bf16[4,80,257]{2,1,0:T(8,128)(2,1)} fusion(bf16[257,4,80]{0,2,1:T(8,128)(2,1)} %bitcast.152, f32[4,257,257]{1,2,0:T(8,128)} %fusion.94, f32[4,257,257]{1,2,0:T(8,128)} %get-tuple-element.20, f32[4,257]{1,0:T(4,128)S(1)} %get-tuple-element.19), kind=kOutput, calls=%fused_computation.38 | convolution fusion | flops 44204256 | bytes 2446640 | tf_op jit(solution)/shard_map/bhqk,bqhe->bkhe/dot_general | solution.py:315
  43.4 4.6 %fusion.45 = bf16[4,80,257]{2,1,0:T(8,128)(2,1)} fusion(bf16[257,4,80]{0,2,1:T(8,128)(2,1)} %bitcast.156, f32[4,257,257]{1,2,0:T(8,128)} %fusion.94, f32[4,257,257]{1,2,0:T(8,128)} %get-tuple-element.20, f32[4,257]{1,0:T(4,128)S(1)} %get-tuple-element.19), kind=kOutput, calls=%fused_computation.37 | convolution fusion | flops 44204256 | bytes 2446640 | tf_op jit(solution)/shard_map/bhqk,bkhe->bqhe/dot_general | solution.py:312
  48.0 1.5 fusion.56
  52.3 2.8 %convolution_add_fusion.2.part = f32[257,1280]{1,0:T(8,128)} fusion(f32[257,1280]{1,0:T(8,128)S(1)} %convolution_add_fusion.3, bf16[257,320]{0,1:T(8,128)(2,1)S(1)} %bitcast.149, bf16[3,1280,320]{1,2,0:T(8,128)(2,1)} %param.6), kind=kOutput, calls=%fused_computation.7 | convolution fusion | flops 210863360 | bytes 3615360 | tf_op jit(solution)/shard_map/dot_general | solution.py:328
  55.1 15.9 %reduce_mid.1 = bf16[257,1280]{1,0:T(8,128)(2,1)} custom-call(f32[257,1280]{1,0:T(8,128)} %convolution_add_fusion.2.part, f32[257,1280]{1,0:T(8,128)} %get-tuple-element.11.nf, f32[257,1]{1,0:T(8,128)} %get-tuple-element.12.inv, bf16[257,1280]{1,0:T(8,128)(2,1)} %get-tuple-element.10.cb), custom_call_target="tpu_custom_call" | custom-call | tf_op jit(solution)/shard_map/reduce_mid/pallas_call | solution.py:178
  71.0 1.6 convolution_convert_fusion.9
  73.2 1.6 fusion.95
  74.9 3.8 %fusion.42 = bf16[4,80,257]{2,1,0:T(8,128)(2,1)S(1)} fusion(bf16[257,4,80]{0,2,1:T(8,128)(2,1)S(1)} %bitcast.154, f32[4,257,257]{1,2,0:T(8,128)} %fusion.95, f32[4,257,257]{1,2,0:T(8,128)} %get-tuple-element.20, f32[4,257]{1,0:T(4,128)S(1)} %get-tuple-element.19), kind=kOutput, calls=%fused_computation.36 | convolution fusion | flops 44204256 | bytes 2446640 | tf_op jit(solution)/shard_map/bhqk,bqhe->bkhe/dot_general | solution.py:315
  78.7 3.8 %fusion.39 = bf16[4,80,257]{2,1,0:T(8,128)(2,1)S(1)} fusion(bf16[257,4,80]{0,2,1:T(8,128)(2,1)S(1)} %bitcast.157, f32[4,257,257]{1,2,0:T(8,128)} %fusion.95, f32[4,257,257]{1,2,0:T(8,128)} %get-tuple-element.20, f32[4,257]{1,0:T(4,128)S(1)} %get-tuple-element.19), kind=kOutput, calls=%fused_computation.35 | convolution fusion | flops 44204256 | bytes 2446640 | tf_op jit(solution)/shard_map/bhqk,bkhe->bqhe/dot_general | solution.py:312
  82.4 1.7 fusion.54
  84.1 1.7 convolution_add_fusion.1
  85.8 2.9 %convolution_add_fusion.part = f32[257,1280]{1,0:T(8,128)} fusion(f32[257,1280]{1,0:T(8,128)S(1)} %convolution_add_fusion.1, bf16[257,320]{0,1:T(8,128)(2,1)S(1)} %bitcast.147, bf16[3,1280,320]{1,2,0:T(8,128)(2,1)} %param.6), kind=kOutput, calls=%fused_computation.5 | convolution fusion | flops 210863360 | bytes 3615360 | tf_op jit(solution)/shard_map/dot_general | solution.py:328
  88.8 16.0 %reduce_last.1 = (bf16[257,1280]{1,0:T(8,128)(2,1)}, f32[257,1280]{1,0:T(8,128)}) custom-call(f32[257,1280]{1,0:T(8,128)} %convolution_add_fusion.part, f32[257,1280]{1,0:T(8,128)} %get-tuple-element.11.nf, f32[257,1]{1,0:T(8,128)} %get-tuple-element.12.inv, bf16[257,1280]{1,0:T(8,128)(2,1)} %get-tuple-element.10.cb), custom_call_target="tpu_custom_call" | custom-call | tf_op jit(solution)/shard_map/reduce_last/pallas_call | solution.py:178
  104.8 1.6 convolution_convert_fusion.8
  107.3 1.6 fusion.96
  109.0 4.5 %fusion.33 = bf16[4,80,257]{2,1,0:T(8,128)(2,1)} fusion(bf16[257,4,80]{0,2,1:T(8,128)(2,1)S(1)} %bitcast.158, f32[4,257,257]{1,2,0:T(8,128)} %fusion.96, f32[4,257,257]{1,2,0:T(8,128)} %get-tuple-element.20, f32[4,257]{1,0:T(4,128)S(1)} %get-tuple-element.19), kind=kOutput, calls=%fused_computation.33 | convolution fusion | flops 44204256 | bytes 2446640 | tf_op jit(solution)/shard_map/bhqk,bkhe->bqhe/dot_general | solution.py:312
  113.5 1.5 convolution_convert_fusion.3
  115.1 4.5 %fusion.36 = bf16[4,80,257]{2,1,0:T(8,128)(2,1)} fusion(bf16[257,4,80]{0,2,1:T(8,128)(2,1)} %bitcast.153, f32[4,257,257]{1,2,0:T(8,128)} %fusion.96, f32[4,257,257]{1,2,0:T(8,128)} %get-tuple-element.20, f32[4,257]{1,0:T(4,128)S(1)} %get-tuple-element.19), kind=kOutput, calls=%fused_computation.34 | convolution fusion | flops 44204256 | bytes 2446640 | tf_op jit(solution)/shard_map/bhqk,bqhe->bkhe/dot_general | solution.py:315
  119.6 1.6 convolution_convert_fusion.2
  123.3 1.9 pad_maximum_fusion
  125.2 5.7 %copy.52 = bf16[1280,1280]{1,0:T(8,128)(2,1)} copy(bf16[1280,1280]{0,1:T(8,128)(2,1)} %pad_maximum_fusion) | data formatting | bytes 6553600 | tf_op jit(solution)/shard_map/concatenate | solution.py:342
  130.9 66.3 %scatter_dp.1 = f32[160,1280]{1,0:T(8,128)} custom-call(bf16[2,2,2,160,1280]{4,3,2,1,0:T(8,128)(2,1)} %bitcast.135), custom_call_target="tpu_custom_call" | custom-call | tf_op jit(solution)/shard_map/scatter_dp/pallas_call | solution.py:265
  197.2 2.2 %slice_bitcast_fusion = (f32[320,160]{0,1:T(8,128)}, f32[1,160,320]{2,1,0:T(8,128)S(1)}, f32[1,160,320]{2,1,0:T(8,128)S(1)}, f32[1,160,320]{2,1,0:T(8,128)S(1)}) fusion(f32[160,1280]{1,0:T(8,128)} %scatter_dp.1), kind=kLoop, calls=%fused_computation.79 | loop fusion | bytes 1638400 | tf_op jit(solution)/shard_map/transpose | solution.py:346
  (42 shorter events, 12.8 us)
Async XLA Ops:
  0.6 31.5 %copy-start = (bf16[320,1280]{1,0:T(8,128)(2,1)S(1)}, bf16[320,1280]{1,0:T(8,128)(2,1)}, u32[]{:S(2)}) copy-start(bf16[320,1280]{1,0:T(8,128)(2,1)} %param.7) | copy-start | bytes 2457604
  2.5 19.9 %copy-start.1 = (bf16[3,1280,320]{1,2,0:T(8,128)(2,1)S(1)}, bf16[3,1280,320]{1,2,0:T(8,128)(2,1)}, u32[]{:S(2)}) copy-start(bf16[3,1280,320]{1,2,0:T(8,128)(2,1)} %param.6) | copy-start | bytes 7372804
  25.8 2.9 %copy-start.9 = (bf16[257,320]{0,1:T(8,128)(2,1)}, bf16[257,320]{0,1:T(8,128)(2,1)S(1)}, u32[]{:S(2)}) copy-start(bf16[257,320]{0,1:T(8,128)(2,1)S(1)} %copy.37) | copy-start | bytes 493444
  48.0 1.5 copy-start.12
  49.5 1.4 copy-start.6
  51.0 0.9 copy-start.5
  72.8 2.1 %copy-start.10 = (bf16[257,320]{0,1:T(8,128)(2,1)S(1)}, bf16[257,320]{0,1:T(8,128)(2,1)}, u32[]{:S(2)}) copy-start(bf16[257,320]{0,1:T(8,128)(2,1)} %copy-done.9) | copy-start | bytes 493444
  74.9 3.8 %copy-start.11 = (bf16[257,320]{0,1:T(8,128)(2,1)S(1)}, bf16[257,320]{0,1:T(8,128)(2,1)}, u32[]{:S(2)}) copy-start(bf16[257,320]{0,1:T(8,128)(2,1)} %copy.36) | copy-start | bytes 493444
  106.6 0.7 copy-start.3
  109.0 4.5 %copy-start.2 = (bf16[257,1280]{1,0:T(8,128)(2,1)S(1)}, bf16[257,1280]{1,0:T(8,128)(2,1)}, u32[]{:S(2)}) copy-start(bf16[257,1280]{1,0:T(8,128)(2,1)} %get-tuple-element.9) | copy-start | bytes 1973764
  119.6 1.6 copy-start.4
  121.6 1.1 copy-start.8
  199.4 2.1 %copy-start.7 = (f32[1,257,320]{2,0,1:T(1,128)S(1)}, f32[1,257,320]{2,0,1:T(1,128)}, u32[]{:S(2)}) copy-start(f32[1,257,320]{2,0,1:T(1,128)} %param.5) | copy-start | bytes 986884

commit v2 on v1

--- a/solution.py
+++ b/solution.py
@@ -111,7 +111,7 @@
 
 def reduce_kernel(last, part, nf, inv, cb, *refs):
     if last:
-        ub_ref, term_ref, a_in, acc, b_out, b_in, c_out, c_in, total, send, recv = refs
+        cot, ub_ref, out_ref, a_in, acc, b_out, b_in, c_out, c_in, total, term_ref, send, recv = refs
     else:
         ub_ref, a_in, acc, b_out, b_in, c_out, c_in, total, send, recv = refs
     me, core, other, across = mp_partners()
@@ -163,32 +163,43 @@
         if last:
             term_ref[:, here] = term
         ub_ref[:, here] = (cb[:, here].astype(jnp.float32) + term).astype(jnp.bfloat16)
+    if last:
+        narrow = out_ref.shape[1]
+        for s in range(4):
+
+            @pl.when(me == s)
+            def _(s=s):
+                out_ref[...] = cot[...] + term_ref[:, s * narrow : (s + 1) * narrow]
+
     for copy in first + second + third:
         copy.wait_send()
 
 
-def reduce_norm(part, nf, inv, cb, last, ident):
+def reduce_norm(part, nf, inv, cb, cot, last, ident):
     tokens, width = part.shape
     pieces = width // 2 // LANES
     shapes = [jax.ShapeDtypeStruct((tokens, width), jnp.bfloat16)]
     if last:
-        shapes.append(jax.ShapeDtypeStruct((tokens, width), jnp.float32))
+        shapes.append(jax.ShapeDtypeStruct(cot.shape, jnp.float32))
     wide = pltpu.VMEM((pieces, tokens, LANES), jnp.float32)
     slim = pltpu.VMEM((pieces, tokens, LANES), jnp.bfloat16)
     return pl.pallas_call(
         functools.partial(reduce_kernel, last),
         name="reduce_last" if last else "reduce_mid",
         out_shape=tuple(shapes),
-        in_specs=vmem(4),
+        in_specs=vmem(5 if last else 4),
         out_specs=tuple(vmem(len(shapes))),
         scratch_shapes=[
             wide, wide, slim, slim, slim, slim,
             pltpu.VMEM((2 * pieces, tokens, LANES), jnp.float32),
+        ]
+        + ([pltpu.VMEM((tokens, width), jnp.float32)] if last else [])
+        + [
             pltpu.SemaphoreType.DMA((3, pieces)),
             pltpu.SemaphoreType.DMA((3, pieces)),
         ],
         compiler_params=pltpu.CompilerParams(collective_id=ident, has_side_effects=True),
-    )(part, nf, inv, cb)
+    )(*((part, nf, inv, cb, cot) if last else (part, nf, inv, cb)))
 
 
 def scatter_kernel(bits, chunks, factor, g_ref, out_ref, *scratch):
@@ -255,7 +266,7 @@
     bits = ranks.bit_length() - 1
     height, width = g.shape
     block = height // ranks
-    chunks = 10 if block % 160 == 0 else 1
+    chunks = 5 if block % 160 == 0 else 1
     rows = block // chunks
     scratch = []
     for s in range(bits):
@@ -274,72 +285,145 @@
     )(g.reshape((2,) * bits + (block, width)))
 
 
+def dot_nt(a, b):
+    return lax.dot_general(a, b, (((1,), (1,)), ((), ())), preferred_element_type=jnp.float32)
+
+
+def dot_tn(a, b):
+    return lax.dot_general(a, b, (((0,), (0,)), ((), ())), preferred_element_type=jnp.float32)
+
+
+def windows(columns):
+    for h in range(columns // HD):
+        low = h * HD // LANES * LANES
+        high = min(-(-(h + 1) * HD // LANES) * LANES, columns)
+        yield h, slice(low, high), h * HD - low
+
+
+def only_head(value, start):
+    lane = lax.broadcasted_iota(jnp.int32, value.shape, 1)
+    return jnp.where((lane >= start) & (lane < start + HD), value, jnp.zeros_like(value))
+
+
+def forward_step(nb, w, q, k, v, probs, att, hold):
+    scale = HD ** (-0.5)
+    normal = nb[...]
+    for c, ref in enumerate((q, k, v)):
+        made = jnp.dot(normal, w[c], preferred_element_type=jnp.float32)
+        ref[...] = made.astype(jnp.bfloat16)
+    hold[...] = jnp.zeros_like(hold)
+    for h, here, start in windows(q.shape[1]):
+        scores = dot_nt(only_head(q[:, here], start), k[:, here]) * scale
+        raised = jnp.exp(scores - jnp.max(scores, axis=-1, keepdims=True))
+        share = raised / jnp.sum(raised, axis=-1, keepdims=True)
+        probs[h] = share
+        hold[:, here] += jnp.dot(
+            share.astype(jnp.bfloat16),
+            only_head(v[:, here], start),
+            preferred_element_type=jnp.float32,
+        )
+    att[...] = hold[...].astype(jnp.bfloat16)
+
+
+def pull_step(rows, wo, q, k, v, probs, holds):
+    scale = HD ** (-0.5)
+    grad = dot_nt(rows[...], wo[...]).astype(jnp.bfloat16)
+    for ref in holds:
+        ref[...] = jnp.zeros_like(ref)
+    for h, here, start in windows(q.shape[1]):
+        own = only_head(grad[:, here], start)
+        pg = dot_nt(own, v[:, here])
+        share = probs[h]
+        rowdot = jnp.sum(share * pg, axis=-1, keepdims=True)
+        sg = (share * (pg - rowdot) * scale).astype(jnp.bfloat16)
+        holds[0][:, here] += jnp.dot(
+            sg, only_head(k[:, here], start), preferred_element_type=jnp.float32
+        )
+        holds[1][:, here] += dot_tn(sg, only_head(q[:, here], start))
+        holds[2][:, here] += dot_tn(share.astype(jnp.bfloat16), own)
+    return [ref[...].astype(jnp.bfloat16) for ref in holds]
+
+
+def back_to_input(grads, w, part):
+    part[...] = dot_nt(grads[0], w[0])
+    part[...] += dot_nt(grads[1], w[1])
+    part[...] += dot_nt(grads[2], w[2])
+
+
+def first_kernel(nb, rows, w, wo, q, k, v, probs, att, part, *holds):
+    forward_step(nb, w, q, k, v, probs, att, holds[0])
+    back_to_input(pull_step(rows, wo, q, k, v, probs, holds), w, part)
+
+
+def middle_kernel(rows, w, wo, q, k, v, probs, part, *holds):
+    back_to_input(pull_step(rows, wo, q, k, v, probs, holds), w, part)
+
+
+def final_kernel(rows, nb, wo, q, k, v, probs, att, g, *holds):
+    side = holds[3]
+    grads = pull_step(rows, wo, q, k, v, probs, holds[:3])
+    columns = q.shape[1]
+    for c, item in enumerate(grads + [att[...]]):
+        side[:, c * columns : (c + 1) * columns] = item
+    cut = 3 * columns
+    low, high = cut // LANES * LANES, -(-cut // LANES) * LANES
+    height = g.shape[0]
+    step = 256 if height % 256 == 0 else height
+    for i in range(height // step):
+        here = slice(i * step, (i + 1) * step)
+        left = dot_tn(nb[:, here], side[:, :high])
+        right = dot_tn(rows[:, here], side[:, low:])
+        g[here, :low] = left[:, :low].astype(jnp.bfloat16)
+        if high > low:
+            lane = lax.broadcasted_iota(jnp.int32, (step, high - low), 1)
+            mixed = jnp.where(lane < cut - low, left[:, low:], right[:, : high - low])
+            g[here, low:high] = mixed.astype(jnp.bfloat16)
+        g[here, high:] = right[:, high - low :].astype(jnp.bfloat16)
+
+
+def local(body, name, shapes, arrays, scratch, flops):
+    return pl.pallas_call(
+        body,
+        name=name,
+        out_shape=tuple(shapes),
+        in_specs=vmem(len(arrays)),
+        out_specs=tuple(vmem(len(shapes))),
+        scratch_shapes=scratch,
+        cost_estimate=pl.CostEstimate(flops=flops, bytes_accessed=4 << 20, transcendentals=0),
+    )(*arrays)
+
+
 def shards(z_star, cotangent, w_qkv, w_out):
     ranks = lax.axis_size("dp")
     images, tokens, narrow = z_star.shape
     columns = w_qkv.shape[2]
+    width = w_qkv.shape[1]
     heads_here = columns // HD
-    score_scale = HD ** (-0.5)
-    position = lax.axis_index("mp")
-    normal_f, flattened, inv_std, cot_rows = gather(z_star[0], cotangent[0])
-
-    def project(slot_index):
-        result = jnp.dot(flattened, w_qkv[slot_index], preferred_element_type=jnp.float32)
-        return result.astype(jnp.bfloat16).reshape(images, tokens, heads_here, HD)
-
-    queries = project(0)
-    key_vecs = project(1)
-    val_vecs = project(2)
-    scores = (
-        jnp.einsum("bqhe,bkhe->bhqk", queries, key_vecs, preferred_element_type=jnp.float32)
-        * score_scale
+    normal_f, normal_b, inv_std, cot_rows = gather(z_star[0], cotangent[0])
+    flat = jax.ShapeDtypeStruct((tokens, columns), jnp.bfloat16)
+    wide = jax.ShapeDtypeStruct((tokens, width), jnp.float32)
+    shares = jax.ShapeDtypeStruct((heads_here, tokens, tokens), jnp.float32)
+    holds = [pltpu.VMEM((tokens, columns), jnp.float32)] * 3
+    work = 6 * tokens * width * columns
+    q, k, v, probs, att, part = local(
+        first_kernel, "first", (flat, flat, flat, shares, flat, wide),
+        (normal_b, cot_rows, w_qkv, w_out), holds, 3 * work,
     )
-    attn_probs = jax.nn.softmax(scores, axis=-1)
-    probs_b = attn_probs.astype(jnp.bfloat16)
-    attended = jnp.einsum("bhqk,bkhe->bqhe", probs_b, val_vecs, preferred_element_type=jnp.float32)
-    attended = attended.astype(jnp.bfloat16).reshape(-1, columns)
-    contract_first = (((0,), (0,)), ((), ()))
-    contract_second = (((1,), (1,)), ((), ()))
-
-    def pull_back(rows):
-        att_grad = lax.dot_general(rows, w_out, contract_second, preferred_element_type=jnp.float32)
-        att_grad = att_grad.astype(jnp.bfloat16).reshape(images, tokens, heads_here, HD)
-        prob_grad = jnp.einsum(
-            "bqhe,bkhe->bhqk", att_grad, val_vecs, preferred_element_type=jnp.float32
-        )
-        rowdot = jnp.sum(attn_probs * prob_grad, axis=-1, keepdims=True)
-        score_grad = (attn_probs * (prob_grad - rowdot) * score_scale).astype(jnp.bfloat16)
-        q_grad = jnp.einsum(
-            "bhqk,bkhe->bqhe", score_grad, key_vecs, preferred_element_type=jnp.float32
-        ).astype(jnp.bfloat16)
-        k_grad = jnp.einsum(
-            "bhqk,bqhe->bkhe", score_grad, queries, preferred_element_type=jnp.float32
-        ).astype(jnp.bfloat16)
-        v_grad = jnp.einsum(
-            "bhqk,bqhe->bkhe", probs_b, att_grad, preferred_element_type=jnp.float32
-        ).astype(jnp.bfloat16)
-        return [item.reshape(-1, columns) for item in (q_grad, k_grad, v_grad)]
-
     rows = cot_rows
-    term = None
     for term_index in range(TERMS - 1):
-        grads = pull_back(rows)
-        in_part = sum(
-            lax.dot_general(grads[c], w_qkv[c], contract_second, preferred_element_type=jnp.float32)
-            for c in range(3)
-        )
+        if term_index:
+            (part,) = local(
+                middle_kernel, "middle", (wide,), (rows, w_qkv, w_out, q, k, v, probs), holds, 2 * work
+            )
         last = term_index + 2 == TERMS
-        made = reduce_norm(in_part, normal_f, inv_std, cot_rows, last, 1 + term_index)
+        made = reduce_norm(part, normal_f, inv_std, cot_rows, cotangent[0], last, 1 + term_index)
         rows = made[0]
-        if last:
-            term = made[1]
-    implicit = cotangent + lax.dynamic_slice_in_dim(term, position * narrow, narrow, 1)[None]
-    grads = pull_back(rows)
-    pieces = [
-        lax.dot_general(flattened, item, contract_first, preferred_element_type=jnp.float32)
-        for item in grads
-    ] + [lax.dot_general(rows, attended, contract_first, preferred_element_type=jnp.float32)]
-    g = jnp.concatenate([item.astype(jnp.bfloat16) for item in pieces], axis=1)
+    implicit = made[1][None]
+    (g,) = local(
+        final_kernel, "final", (jax.ShapeDtypeStruct((width, 4 * columns), jnp.bfloat16),),
+        (rows, normal_b, w_out, q, k, v, probs, att),
+        holds + [pltpu.VMEM((tokens, 4 * columns), jnp.bfloat16)], 2 * work,
+    )
     factor = 1.0 / math.sqrt(images * ranks * tokens)
     block = scatter(g, ranks, factor)
     grad_qkv = jnp.stack([block[:, c * columns : (c + 1) * columns] for c in range(3)])

time: 204 us -> 146 us (0.72)
  matrix products: 63.7 us -> 0 us
  Pallas kernels: 115 us -> 132 us
  local copies, waits for them, and re-layouts: 18.5 us -> 11.4 us
  other arithmetic: 4.24 us -> 0.91 us
    dot_general x29 -> x0, matrix products: 60.8 us -> none  [the longest x3 12.9 us: pull_back(): jnp.einsum('bhqk,bqhe->bkhe', score_grad, queries, preferred_element_type...]
    pallas_call x0 -> x3, Pallas kernels: none -> 27 us  [local(): pl.pallas_call(body, name=name, out_shape=tuple(shapes), in_specs=vmem(le...]
    pallas_call x1, Pallas kernels: 66.3 us -> 56.2 us  [scatter(): pl.pallas_call(functools.partial(scatter_kernel, bits, chunks, factor), n...]
    concatenate x1 -> x0, local copies, waits for them, and re-layouts: 5.66 us -> none  [shards(): g = jnp.concatenate([item.astype(jnp.bfloat16) for item in pieces], axis=1)]
    convert_element_type x6 -> x0, local copies, waits for them, and re-layouts: 5.25 us -> none  [the longest x3 3.08 us: project(): return result.astype(jnp.bfloat16).reshape(images, tokens, heads_here, HD)]
    unnamed x27 -> x3, local copies, waits for them, and re-layouts: 4.23 us -> 9.2 us
    sub x1 -> x0, matrix products: 2.93 us -> none  [shards(): attn_probs = jax.nn.softmax(scores, axis=-1)]
where the time goes in v2:
time: 146 us; the launch traced here: 145 us
  Pallas kernels  132 us (90%)
  local copies, waits for them, and re-layouts  11.4 us (8%)
    pallas_call x1, Pallas kernels, scatter(): pl.pallas_call(functools.partial(scatter_kernel, bits, chunks, factor), n...  56.2 us
    pallas_call x2, Pallas kernels, reduce_norm(): pl.pallas_call(functools.partial(reduce_kernel, last), name='reduce_last'...  32 us
    pallas_call x3, Pallas kernels, local(): pl.pallas_call(body, name=name, out_shape=tuple(shapes), in_specs=vmem(le...  27 us
    pallas_call x1, Pallas kernels, gather(): pl.pallas_call(gather_kernel, name='gather_mp', out_shape=(jax.ShapeDtype...  17 us
    unnamed x3, local copies, waits for them, and re-layouts  9.2 us

profile of v2, /device:TPU:0, one launch (start us, length us, event | category | flops | bytes accessed | tf_op | source)
XLA Modules:
  0.0 145.2 jit_solution(1126288190360526392)
XLA Ops:
  0.6 1.8 %copy.12 = f32[1,257,320]{2,1,0:T(8,128)} copy(f32[1,257,320]{2,0,1:T(1,128)} %param.5) | data formatting | bytes 657920
  2.4 17.0 %gather_mp.1 = (f32[257,1280]{1,0:T(8,128)}, bf16[257,1280]{1,0:T(8,128)(2,1)}, f32[257,1]{1,0:T(8,128)}, bf16[257,1280]{1,0:T(8,128)(2,1)}) custom-call(bf16[257,320]{1,0:T(8,128)(2,1)} %bitcast.18, f32[257,320]{1,0:T(8,128)} %bitcast.15), custom_call_target="tpu_custom_call" | custom-call | tf_op jit(solution)/shard_map/gather_mp/pallas_call | solution.py:90
  19.4 5.3 %copy.7.w = bf16[3,1280,320]{2,1,0:T(8,128)(2,1)} copy(bf16[3,1280,320]{1,2,0:T(8,128)(2,1)} %param.6) | data formatting | bytes 4915200 | tf_op args[2]
  24.7 9.9 %first.1 = (bf16[257,320]{1,0:T(8,128)(2,1)}, bf16[257,320]{1,0:T(8,128)(2,1)}, bf16[257,320]{1,0:T(8,128)(2,1)}, f32[4,257,257]{2,1,0:T(8,128)}, bf16[257,320]{1,0:T(8,128)(2,1)}, /*index=5*/f32[257,1280]{1,0:T(8,128)}) custom-call(bf16[257,1280]{1,0:T(8,128)(2,1)} %get-tuple-element.15.nb, bf16[257,1280]{1,0:T(8,128)(2,1)} %get-tuple-element.16.rows.cb, ...), custom_call_target="tpu_custom_call" | custom-call | flops 1894809600 | bytes 4194304 | tf_op jit(solution)/shard_map/first/pallas_call | solution.py:385
  34.6 15.9 %reduce_mid.1.rows = bf16[257,1280]{1,0:T(8,128)(2,1)} custom-call(f32[257,1280]{1,0:T(8,128)} %get-tuple-element.17.part, f32[257,1280]{1,0:T(8,128)} %get-tuple-element.18.nf, f32[257,1]{1,0:T(8,128)} %get-tuple-element.19.inv, bf16[257,1280]{1,0:T(8,128)(2,1)} %get-tuple-element.16.rows.cb), custom_call_target="tpu_custom_call" | custom-call | tf_op jit(solution)/shard_map/reduce_mid/pallas_call | solution.py:186
  50.5 8.2 %middle.1.part = f32[257,1280]{1,0:T(8,128)} custom-call(bf16[257,1280]{1,0:T(8,128)(2,1)} %reduce_mid.1.rows, bf16[3,1280,320]{2,1,0:T(8,128)(2,1)} %copy.7.w, bf16[320,1280]{1,0:T(8,128)(2,1)} %wo.5, bf16[257,320]{1,0:T(8,128)(2,1)} %get-tuple-element.20.q, bf16[257,320]{1,0:T(8,128)(2,1)} %get-tuple-element.21.k, bf16[257,320]{1,0:T(8,128)(2,1)} %get-tuple-element.22.v, ...), custom_call_target="tpu_custom_call" | custom-call | flops 1263206400 | bytes 4194304 | tf_op jit(solution)/shard_map/middle/pallas_call | solution.py:385
  58.7 16.1 %reduce_last.1 = (bf16[257,1280]{1,0:T(8,128)(2,1)}, f32[257,320]{1,0:T(8,128)}) custom-call(f32[257,1280]{1,0:T(8,128)} %middle.1.part, f32[257,1280]{1,0:T(8,128)} %get-tuple-element.18.nf, f32[257,1]{1,0:T(8,128)} %get-tuple-element.19.inv, bf16[257,1280]{1,0:T(8,128)(2,1)} %get-tuple-element.16.rows.cb, f32[257,320]{1,0:T(8,128)} %bitcast.16), custom_call_target="tpu_custom_call" | custom-call | tf_op jit(solution)/shard_map/reduce_last/pallas_call | solution.py:186
  74.8 2.2 %copy.9 = f32[1,257,320]{2,0,1:T(1,128)} copy(f32[1,257,320]{2,1,0:T(8,128)} %bitcast.17) | data formatting | bytes 657920
  77.0 8.9 %final.1 = bf16[1280,1280]{1,0:T(8,128)(2,1)} custom-call(bf16[257,1280]{1,0:T(8,128)(2,1)} %get-tuple-element.25.rows, bf16[257,1280]{1,0:T(8,128)(2,1)} %get-tuple-element.15.nb, bf16[320,1280]{1,0:T(8,128)(2,1)} %wo.5, bf16[257,320]{1,0:T(8,128)(2,1)} %get-tuple-element.20.q, bf16[257,320]{1,0:T(8,128)(2,1)} %get-tuple-element.21.k, ...), custom_call_target="tpu_custom_call" | custom-call | flops 1263206400 | bytes 4194304 | tf_op jit(solution)/shard_map/final/pallas_call | solution.py:385
  85.9 56.2 %scatter_dp.1 = f32[160,1280]{1,0:T(8,128)} custom-call(bf16[2,2,2,160,1280]{4,3,2,1,0:T(8,128)(2,1)} %bitcast.14), custom_call_target="tpu_custom_call" | custom-call | tf_op jit(solution)/shard_map/scatter_dp/pallas_call | solution.py:276
  142.1 2.2 %slice_bitcast_fusion = (f32[320,160]{0,1:T(8,128)}, f32[1,160,320]{2,1,0:T(8,128)S(1)}, f32[1,160,320]{2,1,0:T(8,128)S(1)}, f32[1,160,320]{2,1,0:T(8,128)S(1)}) fusion(f32[160,1280]{1,0:T(8,128)} %scatter_dp.1), kind=kLoop, calls=%fused_computation.2 | loop fusion | bytes 1638400 | tf_op jit(solution)/shard_map/transpose | solution.py:430
  144.3 0.9 pad_maximum_fusion

commit v3 on v2

--- a/solution.py
+++ b/solution.py
@@ -202,7 +202,7 @@
     )(*((part, nf, inv, cb, cot) if last else (part, nf, inv, cb)))
 
 
-def scatter_kernel(bits, chunks, factor, g_ref, out_ref, *scratch):
+def scatter_kernel(bits, chunks, factor, g_ref, qkv_ref, out_ref, *scratch):
     send, recv = scratch[-2:]
     bufs = scratch[:-2]
     me = lax.axis_index("dp")
@@ -246,7 +246,12 @@
         kept = pick(ref, left, b, mine[b], extra)[...].astype(jnp.float32)
         summed = kept + bufs[s * 2][j].astype(jnp.float32)
         if s == bits - 1:
-            out_ref[j * rows : (j + 1) * rows, :] = summed * factor
+            here = slice(j * rows, (j + 1) * rows)
+            columns = out_ref.shape[1]
+            scaled = summed * factor
+            for c in range(3):
+                qkv_ref[c, here, :] = scaled[:, c * columns : (c + 1) * columns]
+            out_ref[here, :] = scaled[:, 3 * columns :]
         else:
             bufs[s * 2 + 1][j] = summed.astype(jnp.bfloat16)
             begin(j, s + 1)
@@ -276,9 +281,12 @@
     return pl.pallas_call(
         functools.partial(scatter_kernel, bits, chunks, factor),
         name="scatter_dp",
-        out_shape=jax.ShapeDtypeStruct((block, width), jnp.float32),
+        out_shape=(
+            jax.ShapeDtypeStruct((3, block, width // 4), jnp.float32),
+            jax.ShapeDtypeStruct((block, width // 4), jnp.float32),
+        ),
         in_specs=vmem(1),
-        out_specs=pl.BlockSpec(memory_space=pltpu.VMEM),
+        out_specs=tuple(vmem(2)),
         scratch_shapes=scratch
         + [pltpu.SemaphoreType.DMA((bits, chunks)), pltpu.SemaphoreType.DMA((bits, chunks))],
         compiler_params=pltpu.CompilerParams(collective_id=3, has_side_effects=True),
@@ -309,7 +317,7 @@
     scale = HD ** (-0.5)
     normal = nb[...]
     for c, ref in enumerate((q, k, v)):
-        made = jnp.dot(normal, w[c], preferred_element_type=jnp.float32)
+        made = dot_nt(normal, w[c])
         ref[...] = made.astype(jnp.bfloat16)
     hold[...] = jnp.zeros_like(hold)
     for h, here, start in windows(q.shape[1]):
@@ -345,9 +353,9 @@
 
 
 def back_to_input(grads, w, part):
-    part[...] = dot_nt(grads[0], w[0])
-    part[...] += dot_nt(grads[1], w[1])
-    part[...] += dot_nt(grads[2], w[2])
+    part[...] = jnp.dot(grads[0], w[0], preferred_element_type=jnp.float32)
+    part[...] += jnp.dot(grads[1], w[1], preferred_element_type=jnp.float32)
+    part[...] += jnp.dot(grads[2], w[2], preferred_element_type=jnp.float32)
 
 
 def first_kernel(nb, rows, w, wo, q, k, v, probs, att, part, *holds):
@@ -399,6 +407,7 @@
     columns = w_qkv.shape[2]
     width = w_qkv.shape[1]
     heads_here = columns // HD
+    w_rows = jnp.swapaxes(w_qkv, 1, 2)
     normal_f, normal_b, inv_std, cot_rows = gather(z_star[0], cotangent[0])
     flat = jax.ShapeDtypeStruct((tokens, columns), jnp.bfloat16)
     wide = jax.ShapeDtypeStruct((tokens, width), jnp.float32)
@@ -407,13 +416,13 @@
     work = 6 * tokens * width * columns
     q, k, v, probs, att, part = local(
         first_kernel, "first", (flat, flat, flat, shares, flat, wide),
-        (normal_b, cot_rows, w_qkv, w_out), holds, 3 * work,
+        (normal_b, cot_rows, w_rows, w_out), holds, 3 * work,
     )
     rows = cot_rows
     for term_index in range(TERMS - 1):
         if term_index:
             (part,) = local(
-                middle_kernel, "middle", (wide,), (rows, w_qkv, w_out, q, k, v, probs), holds, 2 * work
+                middle_kernel, "middle", (wide,), (rows, w_rows, w_out, q, k, v, probs), holds, 2 * work
             )
         last = term_index + 2 == TERMS
         made = reduce_norm(part, normal_f, inv_std, cot_rows, cotangent[0], last, 1 + term_index)
@@ -425,9 +434,8 @@
         holds + [pltpu.VMEM((tokens, 4 * columns), jnp.bfloat16)], 2 * work,
     )
     factor = 1.0 / math.sqrt(images * ranks * tokens)
-    block = scatter(g, ranks, factor)
-    grad_qkv = jnp.stack([block[:, c * columns : (c + 1) * columns] for c in range(3)])
-    grad_out = block[:, 3 * columns :].T
+    grad_qkv, turned = scatter(g, ranks, factor)
+    grad_out = turned.T
     return (implicit, grad_qkv, grad_out)
 
 

time: 146 us -> 140 us (0.959)
  local copies, waits for them, and re-layouts: 11.4 us -> 6.69 us
    unnamed x3 -> x6, local copies, waits for them, and re-layouts: 9.2 us -> 6.69 us
    transpose x1 -> x0, local copies, waits for them, and re-layouts: 2.17 us -> none  [shards(): grad_out = block[:, 3 * columns:].T]
where the time goes in v3:
time: 140 us; the launch traced here: 139 us
  Pallas kernels  132 us (94%)
  local copies, waits for them, and re-layouts  6.69 us (5%)
    pallas_call x1, Pallas kernels, scatter(): pl.pallas_call(functools.partial(scatter_kernel, bits, chunks, factor), n...  56.4 us
    pallas_call x2, Pallas kernels, reduce_norm(): pl.pallas_call(functools.partial(reduce_kernel, last), name='reduce_last'...  31.9 us
    pallas_call x3, Pallas kernels, local(): pl.pallas_call(body, name=name, out_shape=tuple(shapes), in_specs=vmem(le...  26.6 us
    pallas_call x1, Pallas kernels, gather(): pl.pallas_call(gather_kernel, name='gather_mp', out_shape=(jax.ShapeDtype...  17 us
    unnamed x6, local copies, waits for them, and re-layouts  6.69 us

profile of v3, /device:TPU:0, one launch (start us, length us, event | category | flops | bytes accessed | tf_op | source)
XLA Modules:
  0.0 139.2 jit_solution(931122707653338557)
XLA Ops:
  0.6 1.8 %copy.10 = f32[1,257,320]{2,1,0:T(8,128)} copy(f32[1,257,320]{2,0,1:T(1,128)} %param.5) | data formatting | bytes 657920
  2.4 17.0 %gather_mp.1 = (f32[257,1280]{1,0:T(8,128)}, bf16[257,1280]{1,0:T(8,128)(2,1)}, f32[257,1]{1,0:T(8,128)}, bf16[257,1280]{1,0:T(8,128)(2,1)}) custom-call(bf16[257,320]{1,0:T(8,128)(2,1)} %bitcast.15, f32[257,320]{1,0:T(8,128)} %bitcast.9), custom_call_target="tpu_custom_call" | custom-call | tf_op jit(solution)/shard_map/gather_mp/pallas_call | solution.py:90
  19.4 9.7 %first.1 = (bf16[257,320]{1,0:T(8,128)(2,1)}, bf16[257,320]{1,0:T(8,128)(2,1)}, bf16[257,320]{1,0:T(8,128)(2,1)}, f32[4,257,257]{2,1,0:T(8,128)}, bf16[257,320]{1,0:T(8,128)(2,1)}, /*index=5*/f32[257,1280]{1,0:T(8,128)}) custom-call(bf16[257,1280]{1,0:T(8,128)(2,1)} %get-tuple-element.17.nb, bf16[257,1280]{1,0:T(8,128)(2,1)} %get-tuple-element.18.rows.cb, ...), custom_call_target="tpu_custom_call" | custom-call | flops 1894809600 | bytes 4194304 | tf_op jit(solution)/shard_map/first/pallas_call | solution.py:393
  29.1 15.9 %reduce_mid.1.rows = bf16[257,1280]{1,0:T(8,128)(2,1)} custom-call(f32[257,1280]{1,0:T(8,128)} %get-tuple-element.19.part, f32[257,1280]{1,0:T(8,128)} %get-tuple-element.20.nf, f32[257,1]{1,0:T(8,128)} %get-tuple-element.21.inv, bf16[257,1280]{1,0:T(8,128)(2,1)} %get-tuple-element.18.rows.cb), custom_call_target="tpu_custom_call" | custom-call | tf_op jit(solution)/shard_map/reduce_mid/pallas_call | solution.py:186
  45.0 8.0 %middle.1.part = f32[257,1280]{1,0:T(8,128)} custom-call(bf16[257,1280]{1,0:T(8,128)(2,1)} %reduce_mid.1.rows, bf16[3,320,1280]{2,1,0:T(8,128)(2,1)} %bitcast.12, bf16[320,1280]{1,0:T(8,128)(2,1)} %wo.5, bf16[257,320]{1,0:T(8,128)(2,1)} %get-tuple-element.22.q, bf16[257,320]{1,0:T(8,128)(2,1)} %get-tuple-element.23.k, bf16[257,320]{1,0:T(8,128)(2,1)} %get-tuple-element.24.v, ...), custom_call_target="tpu_custom_call" | custom-call | flops 1263206400 | bytes 4194304 | tf_op jit(solution)/shard_map/middle/pallas_call | solution.py:393
  53.0 16.1 %reduce_last.1 = (bf16[257,1280]{1,0:T(8,128)(2,1)}, f32[257,320]{1,0:T(8,128)}) custom-call(f32[257,1280]{1,0:T(8,128)} %middle.1.part, f32[257,1280]{1,0:T(8,128)} %get-tuple-element.20.nf, f32[257,1]{1,0:T(8,128)} %get-tuple-element.21.inv, bf16[257,1280]{1,0:T(8,128)(2,1)} %get-tuple-element.18.rows.cb, f32[257,320]{1,0:T(8,128)} %bitcast.10), custom_call_target="tpu_custom_call" | custom-call | tf_op jit(solution)/shard_map/reduce_last/pallas_call | solution.py:186
  69.1 2.2 %copy.7 = f32[1,257,320]{2,0,1:T(1,128)} copy(f32[1,257,320]{2,1,0:T(8,128)} %bitcast.13) | data formatting | bytes 657920
  71.2 8.8 %final.1 = bf16[1280,1280]{1,0:T(8,128)(2,1)} custom-call(bf16[257,1280]{1,0:T(8,128)(2,1)} %get-tuple-element.27.rows, bf16[257,1280]{1,0:T(8,128)(2,1)} %get-tuple-element.17.nb, bf16[320,1280]{1,0:T(8,128)(2,1)} %wo.5, bf16[257,320]{1,0:T(8,128)(2,1)} %get-tuple-element.22.q, bf16[257,320]{1,0:T(8,128)(2,1)} %get-tuple-element.23.k, ...), custom_call_target="tpu_custom_call" | custom-call | flops 1263206400 | bytes 4194304 | tf_op jit(solution)/shard_map/final/pallas_call | solution.py:393
  80.0 56.4 %scatter_dp.1 = (f32[3,160,320]{2,1,0:T(8,128)}, f32[160,320]{1,0:T(8,128)}) custom-call(bf16[2,2,2,160,1280]{4,3,2,1,0:T(8,128)(2,1)} %bitcast.8), custom_call_target="tpu_custom_call" | custom-call | tf_op jit(solution)/shard_map/scatter_dp/pallas_call | solution.py:281
  136.4 0.0 copy-start
  136.5 2.1 %copy.13 = f32[3,160,320]{2,1,0:T(8,128)} copy(f32[3,160,320]{2,1,0:T(8,128)} %get-tuple-element.38) | data formatting | bytes 1228800
  138.5 0.0 copy-done
  138.5 0.7 copy.14
Async XLA Ops:
  136.4 2.1 %copy-start = (f32[160,320]{1,0:T(8,128)S(1)}, f32[160,320]{1,0:T(8,128)}, u32[]{:S(2)}) copy-start(f32[160,320]{1,0:T(8,128)} %get-tuple-element.30) | copy-start | bytes 614404
